TPU v7x, 32 devices: a whole 2x2x4 slice. The times are simulated.
32 devices in a mesh: dp: 8 (over y, x, core), tp: 4 (over z).
Axes of the slice: x: 2, y: 2, z: 4, core: 2. Of those that a mesh axis runs over, the one named last changes fastest.
Arguments:
- inputs: bfloat16 [8, 768, 1280], P('dp', 'tp'), may hold values from -6 to 6
- saved_hidden: bfloat16 [8, 768, 5120], P('dp', None, 'tp'), may hold values from -8 to 8
- upstream: bfloat16 [8, 768, 1280], P('dp', 'tp'), may hold values from -6 to 6
- w_in: bfloat16 [1280, 5120], P(None, 'tp'), may hold values from -0.15625 to 0.15625
- w_out: bfloat16 [5120, 1280], P('tp'), may hold values from -0.078125 to 0.078125
- kernel: float32 [7, 1280], replicated, may hold values from -2 to 2
Outputs:
- grad_inputs: bfloat16 [8, 768, 1280], P('dp', 'tp')
- grad_w_in: float32 [1280, 5120], P(None, 'tp')
- grad_w_out: float32 [5120, 1280], P('tp')
- grad_bias: float32 [5120], P('tp')
- grad_kernel: float32 [7, 1280], replicated
All inputs are finite; a program needn't handle non-finite values.
Results may differ from a plain program's by a relative error of at most 0.02.
Values may be sent and summed in bfloat16 or wider, within the bound.
No kernel may reach another device: no remote copies, remote signals or barrier semaphores. Data moves between devices by JAX's collectives and lax.ppermute only.
A program may use at most 128 MiB of HBM per device.

v0:
```python
import jax
import jax.numpy as jnp
from jax import lax
from jax.sharding import PartitionSpec as P

KW = 7


def with_halo(cells, sides, width):
    for axis, dim in sides:
        count = lax.axis_size(axis)
        ends = count - 1
        head = lax.slice_in_dim(cells, 0, width, axis=dim)
        tail = lax.slice_in_dim(cells, cells.shape[dim] - width, cells.shape[dim], axis=dim)
        cells = jnp.concatenate(
            [
                lax.ppermute(tail, axis, [(i, (i + 1) % count) for i in range(ends)]),
                cells,
                lax.ppermute(head, axis, [((i + 1) % count, i) for i in range(ends)]),
            ],
            axis=dim,
        )
    return cells


def gelu_exact(value):
    return jax.nn.gelu(value, approximate=False)


def convolve(padded, kernel, length):
    mixed = padded[3 : 3 + length].astype(jnp.float32)
    for tap in range(KW):
        mixed = mixed + kernel[tap] * padded[tap : tap + length].astype(jnp.float32)
    return mixed.astype(jnp.bfloat16)


def shards(inputs, saved_hidden, upstream, w_in, w_out, kernel):
    tokens = inputs[0]
    hidden = saved_hidden[0]
    grad_out = upstream[0]
    length = tokens.shape[0]
    piece = lax.all_gather(grad_out, "tp", axis=0, tiled=True)
    hidden_rows = hidden.astype(jnp.float32)
    back_rows = lax.dot_general(
        piece, w_out, (((1,), (1,)), ((), ())), preferred_element_type=jnp.float32
    )
    grad_rows = jax.vjp(gelu_exact, hidden_rows)[1](back_rows)[0].astype(jnp.bfloat16)
    buffer = grad_rows
    activated = gelu_exact(hidden_rows).astype(jnp.bfloat16)
    total = lax.dot_general(
        activated, piece, (((0,), (0,)), ((), ())), preferred_element_type=jnp.float32
    )
    grad_w_out = total
    grad_bias = jnp.sum(buffer.astype(jnp.float32), axis=0)
    summed = lax.psum_scatter(
        lax.dot_general(
            buffer, w_in, (((1,), (1,)), ((), ())), preferred_element_type=jnp.float32
        ).astype(jnp.bfloat16),
        "tp",
        scatter_dimension=0,
        tiled=True,
    ).astype(jnp.float32)
    grad_mixed = (grad_out.astype(jnp.float32) + summed).astype(jnp.bfloat16)
    padded = with_halo(tokens, (("tp", 0),), 3)
    mixed = convolve(padded, kernel, length)
    grad_rows = buffer
    grad_w_in = lax.dot_general(
        lax.all_gather(mixed, "tp", axis=0, tiled=True),
        grad_rows,
        (((0,), (0,)), ((), ())),
        preferred_element_type=jnp.float32,
    )
    grad_pad = with_halo(grad_mixed, (("tp", 0),), 3)
    grad_f = grad_mixed.astype(jnp.float32)
    grad_inputs = grad_f
    taps = []
    for tap in range(KW):
        grad_inputs = grad_inputs + kernel[tap] * grad_pad[6 - tap : 6 - tap + length].astype(
            jnp.float32
        )
        taps.append(jnp.sum(grad_f * padded[tap : tap + length].astype(jnp.float32), axis=0))
    grad_kernel = jnp.stack(taps)
    grad_kernel = lax.psum(grad_kernel, ("dp", "tp"))
    grad_w_in, grad_w_out, grad_bias = (
        lax.psum(grad_w_in.astype(jnp.bfloat16), "dp").astype(jnp.float32),
        lax.psum(grad_w_out.astype(jnp.bfloat16), "dp").astype(jnp.float32),
        lax.psum(grad_bias.astype(jnp.bfloat16), "dp").astype(jnp.float32),
    )
    return (grad_inputs.astype(jnp.bfloat16)[None], grad_w_in, grad_w_out, grad_bias, grad_kernel)


def solution(mesh):
    in_specs = (
        P("dp", "tp", None),
        P("dp", None, "tp"),
        P("dp", "tp", None),
        P(None, "tp"),
        P("tp", None),
        P(),
    )
    out_specs = (P("dp", "tp", None), P(None, "tp"), P("tp", None), P("tp"), P())
    return jax.shard_map(shards, mesh=mesh, in_specs=in_specs, out_specs=out_specs, check_vma=False)
```

profile of v0, /device:TPU:0, one launch (start us, length us, event | category | flops | bytes accessed | tf_op | source)
XLA Modules:
  0.0 318.5 jit_solution(17866380397956469389)
XLA Ops:
  7.2 0.0 copy-start
  7.2 0.0 all-gather.6.cloned.1.call-start
  7.2 0.7 all-gather.6.cloned.1.call-update
  7.9 0.0 all-gather.4.cloned.1.call-start
  8.0 1.0 slice_bitcast_fusion.1
  8.9 5.0 %collective-permute-start.2 = (bf16[3,1280]{1,0:T(4,128)(2,1)S(1)}, bf16[3,1280]{1,0:T(4,128)(2,1)S(1)}, u32[]{:S(2)}, u32[]{:S(2)}) collective-permute-start(bf16[3,1280]{1,0:T(4,128)(2,1)S(1)} %get-tuple-element.27), channel_id=1, source_target_pairs={{0,1},{1,2},{2,3},{4,5},{5,6},{6,7},{8,9},{9,10},{10,11},{12,13},{... | collective-permute-start | bytes 23048 | tf_op jit(solution)/shard_map/ppermute | solution.py:17
  13.9 1.3 collective-permute-start.3
  15.2 1.3 slice_reduce_fusion.6
  16.4 0.0 collective-permute-done.2
  16.5 3.0 collective-permute-done.3
  19.4 4.4 %fusion.52 = bf16[192,1280]{1,0:T(8,128)(2,1)} fusion(bf16[192,1280]{1,0:T(8,128)(2,1)} %bitcast.131, bf16[3,1280]{1,0:T(4,128)(2,1)S(1)} %collective-permute-done.3, bf16[3,1280]{1,0:T(4,128)(2,1)S(1)} %collective-permute-done.2, f32[1280]{0:T(1024)S(1)} %get-tuple-element.20, f32[1280]{0:T(1024)S(1)} %get-tuple-element.21, f32[1280]{0:T(1024)S(1)} %get-tuple-element.16, ...), kind=kLoop, calls=%fused_computation.72 | loop fusion | flops 9830400 | bytes 1034240 | tf_op jit(solution)/shard_map/convert_element_type | solution.py:34
  23.8 0.0 all-gather.4.cloned.1.call-update
  23.9 0.0 all-reduce.3.cloned.1.call-start
  23.9 10.1 %fusion.38 = f32[768,1280]{1,0:T(8,128)} fusion(bf16[1,768,1280]{2,1,0:T(8,128)(2,1)} %param.7), kind=kLoop, calls=%fused_computation.43 | loop fusion | flops 61931520 | bytes 5898240 | tf_op jit(solution)/shard_map/jvp()/erfc | solution.py:27
  34.0 21.8 %all-gather.6.cloned.1.call-done = bf16[1,768,1280]{2,1,0:T(8,128)(2,1)} async-done(((bf16[1,192,1280]{2,1,0:T(8,128)(2,1)}), bf16[1,768,1280]{2,1,0:T(8,128)(2,1)}) %all-gather.6.cloned.1.call-update) | async-done | bytes 1966096 | tf_op jit(solution)/shard_map/all_gather | solution.py:42
  55.8 0.0 copy-start.1
  55.8 0.0 copy-start.4
  55.8 0.0 copy-start.5
  55.8 7.9 %convolution_convert_fusion = bf16[1280,1280]{1,0:T(8,128)(2,1)} fusion(f32[768,1280]{1,0:T(8,128)} %fusion.38, bf16[1,768,1280]{2,1,0:T(8,128)(2,1)} %param.7, bf16[1,768,1280]{2,1,0:T(8,128)(2,1)} %all-gather.6.cloned.1.call-done), kind=kOutput, calls=%fused_computation | convolution fusion | flops 2522152960 | bytes 11141120 | tf_op jit(solution)/shard_map/dot_general | solution.py:50
  63.7 0.0 copy-done
  63.7 0.0 copy-done.1
  63.7 0.0 copy-done.4
  63.7 0.0 copy-done.5
  63.8 4.7 %fusion.80 = (bf16[1280]{0:T(1024)(128)(2,1)S(1)}, bf16[768,1280]{1,0:T(8,128)(2,1)}) fusion(f32[768,1280]{1,0:T(8,128)S(1)} %copy-done.1, bf16[1280,1280]{1,0:T(8,128)(2,1)S(1)} %copy-done, bf16[1,768,1280]{2,1,0:T(8,128)(2,1)S(1)} %copy-done.5, bf16[1,768,1280]{2,1,0:T(8,128)(2,1)S(1)} %copy-done.4), kind=kOutput, calls=%fused_computation.121 | convolution fusion | flops 2532309760 | bytes 13109760 | tf_op jit(solution)/shard_map/dot_general | solution.py:44
  68.5 31.9 %all-gather.4.cloned.1.call-done = bf16[768,1280]{1,0:T(8,128)(2,1)} async-done(((bf16[192,1280]{1,0:T(8,128)(2,1)}), bf16[768,1280]{1,0:T(8,128)(2,1)}) %all-gather.4.cloned.1.call-update) | async-done | bytes 1966096 | tf_op jit(solution)/shard_map/all_gather | solution.py:68
  100.3 6.6 %convolution_convert_fusion.1 = bf16[1280,1280]{1,0:T(8,128)(2,1)} fusion(bf16[768,1280]{1,0:T(8,128)(2,1)} %all-gather.4.cloned.1.call-done, bf16[768,1280]{1,0:T(8,128)(2,1)} %get-tuple-element.30), kind=kOutput, calls=%fused_computation.1 | convolution fusion | flops 2518220800 | bytes 7208960 | tf_op jit(solution)/shard_map/dot_general | solution.py:67
  106.9 0.0 all-reduce.3.cloned.1.call-update
  106.9 0.2 reduce-scatter.2.cloned.1.call-start
  107.2 6.6 %convolution_convert_fusion.2 = bf16[768,1280]{1,0:T(8,128)(2,1)} fusion(bf16[768,1280]{1,0:T(8,128)(2,1)} %get-tuple-element.30, bf16[1280,1280]{1,0:T(8,128)(2,1)} %param.9), kind=kOutput, calls=%fused_computation.44 | convolution fusion | flops 2517565440 | bytes 7208960 | tf_op jit(solution)/shard_map/dot_general | solution.py:56
  113.8 0.0 reduce-scatter.2.cloned.1.call-update
  113.8 14.3 %psum.30 = bf16[1280]{0:T(1024)(128)(2,1)S(1)} all-reduce(bf16[1280]{0:T(1024)(128)(2,1)S(1)} %get-tuple-element.29), channel_id=1, replica_groups=mesh['dp'=8,'tp'=4] {'dp'}, use_global_device_ids=true, to_apply=%region_4.0 | all-reduce | flops 1280 | bytes 5120 | tf_op jit(solution)/shard_map/psum | solution.py:87
  128.1 0.6 convert_element_type.123
  128.7 84.3 %all-reduce.3.cloned.1.call-done = (bf16[1280,1280]{1,0:T(8,128)(2,1)}, bf16[1280,1280]{1,0:T(8,128)(2,1)}) async-done(((bf16[1280,1280]{1,0:T(8,128)(2,1)}, bf16[1280,1280]{1,0:T(8,128)(2,1)}), (bf16[1280,1280]{1,0:T(8,128)(2,1)}, bf16[1280,1280]{1,0:T(8,128)(2,1)})) %all-reduce.3.cloned.1.call-update) | async-done | bytes 6553616 | tf_op jit(solution)/shard_map/psum | solution.py:85
  213.1 0.0 copy-start.2
  213.1 5.4 %convert_element_type.119 = f32[1280,1280]{1,0:T(8,128)} convert(bf16[1280,1280]{1,0:T(8,128)(2,1)} %get-tuple-element.22) | non-fusion elementwise | flops 1638400 | bytes 9830400 | tf_op jit(solution)/shard_map/convert_element_type | solution.py:85
  218.4 0.0 copy-done.2
  218.4 3.3 %convert_element_type.122 = f32[1280,1280]{1,0:T(8,128)} convert(bf16[1280,1280]{1,0:T(8,128)(2,1)S(1)} %copy-done.2) | non-fusion elementwise | flops 1638400 | bytes 9830400 | tf_op jit(solution)/shard_map/convert_element_type | solution.py:86
  221.7 35.3 %reduce-scatter.2.cloned.1.call-done = bf16[192,1280]{1,0:T(8,128)(2,1)} async-done(((bf16[768,1280]{1,0:T(8,128)(2,1)}), bf16[192,1280]{1,0:T(8,128)(2,1)}) %reduce-scatter.2.cloned.1.call-update) | async-done | bytes 491536 | tf_op jit(solution)/shard_map/reduce_scatter | solution.py:55
  257.0 3.8 %fusion.66 = (f32[1280]{0:T(1024)S(1)}, f32[1280]{0:T(1024)S(1)}, f32[1280]{0:T(1024)S(1)}, f32[1280]{0:T(1024)S(1)}, f32[1280]{0:T(1024)S(1)}, /*index=5*/f32[1...) fusion(bf16[3,1280]{1,0:T(4,128)(2,1)S(1)} %collective-permute-done.3, bf16[192,1280]{1,0:T(8,128)(2,1)} %bitcast.132, ...), kind=kLoop, calls=%fused_computation.86 | loop fusion | flops 10804480 | bytes 2508800 | tf_op jit(solution)/shard_map/reduce_sum | solution.py:81
  260.8 0.0 copy-start.3
  260.9 0.7 copy-done.3
  261.6 1.3 collective-permute-start
  262.9 4.5 %collective-permute-start.1 = (bf16[3,1280]{1,0:T(4,128)(2,1)S(1)}, bf16[3,1280]{1,0:T(4,128)(2,1)S(1)}, u32[]{:S(2)}, u32[]{:S(2)}) collective-permute-start(bf16[3,1280]{1,0:T(4,128)(2,1)S(1)} %get-tuple-element.26), channel_id=1, source_target_pairs={{0,1},{1,2},{2,3},{4,5},{5,6},{6,7},{8,9},{9,10},{10,11},{12,13},{... | collective-permute-start | bytes 23048 | tf_op jit(solution)/shard_map/ppermute | solution.py:17
  267.4 0.1 stack.31
  267.5 40.2 %psum.31 = f32[7,1280]{1,0:T(8,128)} all-reduce(f32[7,1280]{1,0:T(8,128)S(1)} %stack.31), channel_id=1, replica_groups=mesh['dp'=8,'tp'=4] {'dp','tp'}, use_global_device_ids=true, to_apply=%region_12.0 | all-reduce | flops 8960 | bytes 71680 | tf_op jit(solution)/shard_map/psum | solution.py:83
  307.6 0.0 collective-permute-done
  307.6 0.0 collective-permute-done.1
  307.6 4.3 %fusion.76 = bf16[1,192,1280]{2,1,0:T(8,128)(2,1)} fusion(bf16[192,1280]{1,0:T(8,128)(2,1)} %copy-done.3, bf16[3,1280]{1,0:T(4,128)(2,1)S(1)} %collective-permute-done.1, f32[1280]{0:T(1024)S(1)} %get-tuple-element.20, f32[1280]{0:T(1024)S(1)} %get-tuple-element.21, f32[1280]{0:T(1024)S(1)} %get-tuple-element.16, f32[1280]{0:T(1024)S(1)} %get-tuple-element.17, ...), kind=kLoop, calls=%fused_computation.109 | loop fusion | flops 9830400 | bytes 1034240 | tf_op jit(solution)/shard_map/broadcast_in_dim | solution.py:89
  (8 shorter events, 0.0 us)
Async XLA Ops:
  7.2 56.6 %copy-start = (bf16[1280,1280]{1,0:T(8,128)(2,1)S(1)}, bf16[1280,1280]{1,0:T(8,128)(2,1)}, u32[]{:S(2)}) copy-start(bf16[1280,1280]{1,0:T(8,128)(2,1)} %param.10) | copy-start | bytes 9830404
  7.2 48.6 %all-gather.6.cloned.1.call-start = ((), (), s32[]{:S(2)}) async-start(), calls=%async_computation.3 | async-start | bytes 2457600 | tf_op jit(solution)/shard_map/all_gather | solution.py:42
  7.9 92.4 %all-gather.4.cloned.1.call-start = ((), (), s32[]{:S(2)}) async-start(), calls=%async_computation.2 | async-start | bytes 2457600 | tf_op jit(solution)/shard_map/all_gather | solution.py:68
  8.9 7.5 %collective-permute-start.2 = (bf16[3,1280]{1,0:T(4,128)(2,1)S(1)}, bf16[3,1280]{1,0:T(4,128)(2,1)S(1)}, u32[]{:S(2)}, u32[]{:S(2)}) collective-permute-start(bf16[3,1280]{1,0:T(4,128)(2,1)S(1)} %get-tuple-element.27), channel_id=1, source_target_pairs={{0,1},{1,2},{2,3},{4,5},{5,6},{6,7},{8,9},{9,10},{10,11},{12,13},{... | collective-permute-start | bytes 23048 | tf_op jit(solution)/shard_map/ppermute | solution.py:17
  13.9 5.6 %collective-permute-start.3 = (bf16[3,1280]{1,0:T(4,128)(2,1)S(1)}, bf16[3,1280]{1,0:T(4,128)(2,1)S(1)}, u32[]{:S(2)}, u32[]{:S(2)}) collective-permute-start(bf16[3,1280]{1,0:T(4,128)(2,1)S(1)} %get-tuple-element.28), channel_id=1, source_target_pairs={{1,0},{2,1},{3,2},{5,4},{6,5},{7,6},{9,8},{10,9},{11,10},{13,12},{... | collective-permute-start | bytes 23048 | tf_op jit(solution)/shard_map/ppermute | solution.py:19
  23.9 189.2 %all-reduce.3.cloned.1.call-start = ((), (), s32[]{:S(2)}) async-start(), calls=%async_computation.4 | async-start | bytes 13107200 | tf_op jit(solution)/shard_map/psum | solution.py:85
  55.8 7.9 %copy-start.1 = (f32[768,1280]{1,0:T(8,128)S(1)}, f32[768,1280]{1,0:T(8,128)}, u32[]{:S(2)}) copy-start(f32[768,1280]{1,0:T(8,128)} %fusion.38) | copy-start | bytes 11796484
  55.8 7.9 %copy-start.4 = (bf16[1,768,1280]{2,1,0:T(8,128)(2,1)S(1)}, bf16[1,768,1280]{2,1,0:T(8,128)(2,1)}, u32[]{:S(2)}) copy-start(bf16[1,768,1280]{2,1,0:T(8,128)(2,1)} %param.7) | copy-start | bytes 5898244
  55.8 7.9 %copy-start.5 = (bf16[1,768,1280]{2,1,0:T(8,128)(2,1)S(1)}, bf16[1,768,1280]{2,1,0:T(8,128)(2,1)}, u32[]{:S(2)}) copy-start(bf16[1,768,1280]{2,1,0:T(8,128)(2,1)} %all-gather.6.cloned.1.call-done) | copy-start | bytes 5898244
  106.9 150.0 %reduce-scatter.2.cloned.1.call-start = ((), (), s32[]{:S(2)}) async-start(), calls=%async_computation.1 | async-start | bytes 2457600 | tf_op jit(solution)/shard_map/reduce_scatter | solution.py:55
  213.1 5.4 %copy-start.2 = (bf16[1280,1280]{1,0:T(8,128)(2,1)S(1)}, bf16[1280,1280]{1,0:T(8,128)(2,1)}, u32[]{:S(2)}) copy-start(bf16[1280,1280]{1,0:T(8,128)(2,1)} %get-tuple-element.23) | copy-start | bytes 9830404
  260.8 0.8 copy-start.3
  261.6 46.1 %collective-permute-start = (bf16[3,1280]{1,0:T(4,128)(2,1)S(1)}, bf16[3,1280]{1,0:T(4,128)(2,1)S(1)}, u32[]{:S(2)}, u32[]{:S(2)}) collective-permute-start(bf16[3,1280]{1,0:T(4,128)(2,1)S(1)} %get-tuple-element.25), channel_id=1, source_target_pairs={{1,0},{2,1},{3,2},{5,4},{6,5},{7,6},{9,8},{10,9},{11,10},{13,12},{... | collective-permute-start | bytes 23048 | tf_op jit(solution)/shard_map/ppermute | solution.py:19
  262.9 44.8 %collective-permute-start.1 = (bf16[3,1280]{1,0:T(4,128)(2,1)S(1)}, bf16[3,1280]{1,0:T(4,128)(2,1)S(1)}, u32[]{:S(2)}, u32[]{:S(2)}) collective-permute-start(bf16[3,1280]{1,0:T(4,128)(2,1)S(1)} %get-tuple-element.26), channel_id=1, source_target_pairs={{0,1},{1,2},{2,3},{4,5},{5,6},{6,7},{8,9},{9,10},{10,11},{12,13},{... | collective-permute-start | bytes 23048 | tf_op jit(solution)/shard_map/ppermute | solution.py:17
Sparse Core Ops, SparseCore 0:
  9.6 46.2 all-gather.5
  58.0 42.3 all-gather.3
  107.1 105.9 all-reduce.2
  215.2 41.6 reduce-scatter.1
where the time goes:
time: 319 us; the launch traced here: 318 us
  waiting for transfers between devices  177 us (55%)
  blocking collectives  54.5 us (17%)
  other arithmetic  31.8 us (10%)
  matrix products  25.8 us (8%)
  between operations  13.9 us (4%)
  starting transfers between devices  12.4 us (4%)
    psum x1, waiting for transfers between devices, shards(): lax.psum(grad_w_in.astype(jnp.bfloat16), 'dp').astype(jnp.float32)  84.3 us
    psum x1, blocking collectives, shards(): grad_kernel = lax.psum(grad_kernel, ('dp', 'tp'))  40.2 us
    reduce_scatter x1, waiting for transfers between devices, shards(): lax.psum_scatter(lax.dot_general(buffer, w_in, (((1,), (1,)), ((), ())),...  35.3 us
    all_gather x1, waiting for transfers between devices, shards(): lax.all_gather(mixed, 'tp', axis=0, tiled=True)  31.9 us
    all_gather x1, waiting for transfers between devices, shards(): piece = lax.all_gather(grad_out, 'tp', axis=0, tiled=True)  21.8 us
    psum x1, blocking collectives, shards(): lax.psum(grad_bias.astype(jnp.bfloat16), 'dp').astype(jnp.float32)  14.3 us
    another operation x1, other arithmetic, gelu_exact(): return jax.nn.gelu(value, approximate=False)  10.1 us
    ppermute x2, starting transfers between devices, with_halo(): lax.ppermute(tail, axis, [(i, (i + 1) % count) for i in range(ends)])  9.5 us
  transfers between devices with their start and end apart: 8, of which 5 were waited for; matrix products, arithmetic and copies ran while one was open for 14% of the time, Pallas kernels for 0%

commit v1 on v0

--- a/solution.py
+++ b/solution.py
@@ -82,7 +82,7 @@
     grad_kernel = jnp.stack(taps)
     grad_kernel = lax.psum(grad_kernel, ("dp", "tp"))
     grad_w_in, grad_w_out, grad_bias = (
-        lax.psum(grad_w_in.astype(jnp.bfloat16), "dp").astype(jnp.float32),
+        jnp.sum(lax.all_gather(grad_w_in.astype(jnp.bfloat16), "dp"), axis=0).astype(jnp.float32),
         lax.psum(grad_w_out.astype(jnp.bfloat16), "dp").astype(jnp.float32),
         lax.psum(grad_bias.astype(jnp.bfloat16), "dp").astype(jnp.float32),
     )

time: 319 us -> 382 us (1.20)
  waiting for transfers between devices: 177 us -> 221 us
  other arithmetic: 31.8 us -> 49.5 us
    all_gather x0 -> x1, waiting for transfers between devices: none -> 80.8 us  [shards(): lax.all_gather(grad_w_in.astype(jnp.bfloat16), 'dp')]
    psum x1, waiting for transfers between devices: 84.3 us -> 51.7 us  [shards(): lax.psum(grad_w_out.astype(jnp.bfloat16), 'dp').astype(jnp.float32)]
    reduce_sum x0 -> x1, other arithmetic: none -> 20.1 us  [shards(): jnp.sum(lax.all_gather(grad_w_in.astype(jnp.bfloat16), 'dp'), axis=0)]
    all_gather x1, waiting for transfers between devices: 31.9 us -> 23.8 us  [shards(): lax.all_gather(mixed, 'tp', axis=0, tiled=True)]
  transfers between devices with their start and end apart: 8 -> 9, of which waited for: 5 -> 6; matrix products, arithmetic and copies ran while one was open for 14% -> 14% of each run, Pallas kernels for 0% -> 0%
where the time goes in v1:
time: 382 us; the launch traced here: 381 us
  waiting for transfers between devices  221 us (58%)
  blocking collectives  55.6 us (15%)
  other arithmetic  49.5 us (13%)
  matrix products  25.7 us (7%)
  between operations  13.9 us (4%)
  starting transfers between devices  12.5 us (3%)
    all_gather x1, waiting for transfers between devices, shards(): lax.all_gather(grad_w_in.astype(jnp.bfloat16), 'dp')  80.8 us
    psum x1, waiting for transfers between devices, shards(): lax.psum(grad_w_out.astype(jnp.bfloat16), 'dp').astype(jnp.float32)  51.7 us
    psum x1, blocking collectives, shards(): grad_kernel = lax.psum(grad_kernel, ('dp', 'tp'))  41.4 us
    reduce_scatter x1, waiting for transfers between devices, shards(): lax.psum_scatter(lax.dot_general(buffer, w_in, (((1,), (1,)), ((), ())),...  38.6 us
    all_gather x1, waiting for transfers between devices, shards(): lax.all_gather(mixed, 'tp', axis=0, tiled=True)  23.8 us
    all_gather x1, waiting for transfers between devices, shards(): piece = lax.all_gather(grad_out, 'tp', axis=0, tiled=True)  21.9 us
    reduce_sum x1, other arithmetic, shards(): jnp.sum(lax.all_gather(grad_w_in.astype(jnp.bfloat16), 'dp'), axis=0)  20.1 us
    psum x1, blocking collectives, shards(): lax.psum(grad_bias.astype(jnp.bfloat16), 'dp').astype(jnp.float32)  14.2 us
  transfers between devices with their start and end apart: 9, of which 6 were waited for; matrix products, arithmetic and copies ran while one was open for 14% of the time, Pallas kernels for 0%

profile of v1, /device:TPU:0, one launch (start us, length us, event | category | flops | bytes accessed | tf_op | source)
XLA Modules:
  0.0 381.4 jit_solution(13089914746992956648)
XLA Ops:
  7.2 0.0 copy-start
  7.2 0.0 all-gather.8.cloned.1.call-start
  7.2 0.7 all-gather.8.cloned.1.call-update
  7.9 0.0 all-gather.6.cloned.1.call-start
  8.0 1.0 slice_bitcast_fusion.1
  8.9 5.0 %collective-permute-start.2 = (bf16[3,1280]{1,0:T(4,128)(2,1)S(1)}, bf16[3,1280]{1,0:T(4,128)(2,1)S(1)}, u32[]{:S(2)}, u32[]{:S(2)}) collective-permute-start(bf16[3,1280]{1,0:T(4,128)(2,1)S(1)} %get-tuple-element.25), channel_id=1, source_target_pairs={{0,1},{1,2},{2,3},{4,5},{5,6},{6,7},{8,9},{9,10},{10,11},{12,13},{... | collective-permute-start | bytes 23048 | tf_op jit(solution)/shard_map/ppermute | solution.py:17
  13.9 1.3 collective-permute-start.3
  15.2 1.3 slice_reduce_fusion.6
  16.4 0.0 collective-permute-done.2
  16.5 3.0 collective-permute-done.3
  19.4 4.3 %fusion.52 = bf16[192,1280]{1,0:T(8,128)(2,1)} fusion(bf16[192,1280]{1,0:T(8,128)(2,1)} %bitcast.133, bf16[3,1280]{1,0:T(4,128)(2,1)S(1)} %collective-permute-done.3, bf16[3,1280]{1,0:T(4,128)(2,1)S(1)} %collective-permute-done.2, f32[1280]{0:T(1024)S(1)} %get-tuple-element.20, f32[1280]{0:T(1024)S(1)} %get-tuple-element.21, f32[1280]{0:T(1024)S(1)} %get-tuple-element.16, ...), kind=kLoop, calls=%fused_computation.72 | loop fusion | flops 9830400 | bytes 1034240 | tf_op jit(solution)/shard_map/convert_element_type | solution.py:34
  23.8 0.0 all-gather.6.cloned.1.call-update
  23.8 0.0 all-reduce.2.cloned.1.call-start
  23.9 10.1 %fusion.38 = f32[768,1280]{1,0:T(8,128)} fusion(bf16[1,768,1280]{2,1,0:T(8,128)(2,1)} %param.7), kind=kLoop, calls=%fused_computation.43 | loop fusion | flops 61931520 | bytes 5898240 | tf_op jit(solution)/shard_map/jvp()/erfc | solution.py:27
  33.9 21.9 %all-gather.8.cloned.1.call-done = bf16[1,768,1280]{2,1,0:T(8,128)(2,1)} async-done(((bf16[1,192,1280]{2,1,0:T(8,128)(2,1)}), bf16[1,768,1280]{2,1,0:T(8,128)(2,1)}) %all-gather.8.cloned.1.call-update) | async-done | bytes 1966096 | tf_op jit(solution)/shard_map/all_gather | solution.py:42
  55.8 7.7 %convolution_convert_fusion = bf16[1280,1280]{1,0:T(8,128)(2,1)} fusion(f32[768,1280]{1,0:T(8,128)} %fusion.38, bf16[1,768,1280]{2,1,0:T(8,128)(2,1)} %param.7, bf16[1,768,1280]{2,1,0:T(8,128)(2,1)} %all-gather.8.cloned.1.call-done), kind=kOutput, calls=%fused_computation | convolution fusion | flops 2522152960 | bytes 11141120 | tf_op jit(solution)/shard_map/dot_general | solution.py:50
  63.6 0.0 all-reduce.2.cloned.1.call-update
  63.6 0.0 reduce-scatter.2.cloned.1.call-start
  63.6 0.0 copy-done
  63.6 0.0 copy-start.4
  63.7 7.5 %fusion.80 = (bf16[1280]{0:T(1024)(128)(2,1)S(1)}, bf16[768,1280]{1,0:T(8,128)(2,1)S(1)}) fusion(f32[768,1280]{1,0:T(8,128)} %fusion.38, bf16[1280,1280]{1,0:T(8,128)(2,1)S(1)} %copy-done, bf16[1,768,1280]{2,1,0:T(8,128)(2,1)} %all-gather.8.cloned.1.call-done, bf16[1,768,1280]{2,1,0:T(8,128)(2,1)} %param.7), kind=kOutput, calls=%fused_computation.121 | convolution fusion | flops 2532309760 | bytes 13109760 | tf_op jit(solution)/shard_map/dot_general | solution.py:44
  71.1 0.0 copy-start.5
  71.1 1.3 copy-done.5
  72.4 0.0 copy-done.4
  72.4 3.9 %convolution_convert_fusion.2 = bf16[768,1280]{1,0:T(8,128)(2,1)} fusion(bf16[768,1280]{1,0:T(8,128)(2,1)S(1)} %get-tuple-element.28, bf16[1280,1280]{1,0:T(8,128)(2,1)S(1)} %copy-done.4), kind=kOutput, calls=%fused_computation.44 | convolution fusion | flops 2517565440 | bytes 7208960 | tf_op jit(solution)/shard_map/dot_general | solution.py:56
  76.3 0.0 reduce-scatter.2.cloned.1.call-update
  76.3 0.2 all-gather.10.cloned.1.call-start
  76.6 23.8 %all-gather.6.cloned.1.call-done = bf16[768,1280]{1,0:T(8,128)(2,1)} async-done(((bf16[192,1280]{1,0:T(8,128)(2,1)}), bf16[768,1280]{1,0:T(8,128)(2,1)}) %all-gather.6.cloned.1.call-update) | async-done | bytes 1966096 | tf_op jit(solution)/shard_map/all_gather | solution.py:68
  100.3 6.6 %convolution_convert_fusion.1 = bf16[1280,1280]{1,0:T(8,128)(2,1)} fusion(bf16[768,1280]{1,0:T(8,128)(2,1)} %all-gather.6.cloned.1.call-done, bf16[768,1280]{1,0:T(8,128)(2,1)} %copy-done.5), kind=kOutput, calls=%fused_computation.1 | convolution fusion | flops 2518220800 | bytes 7208960 | tf_op jit(solution)/shard_map/dot_general | solution.py:67
  106.9 0.0 all-gather.10.cloned.1.call-update
  107.0 14.2 %psum.22 = bf16[1280]{0:T(1024)(128)(2,1)S(1)} all-reduce(bf16[1280]{0:T(1024)(128)(2,1)S(1)} %get-tuple-element.27), channel_id=1, replica_groups=mesh['dp'=8,'tp'=4] {'dp'}, use_global_device_ids=true, to_apply=%region_4.0 | all-reduce | flops 1280 | bytes 5120 | tf_op jit(solution)/shard_map/psum | solution.py:87
  121.2 0.6 convert_element_type.125
  121.8 0.0 copy-start.2
  121.8 0.0 copy-start.3
  121.8 51.7 %all-reduce.2.cloned.1.call-done = bf16[1280,1280]{1,0:T(8,128)(2,1)} async-done(((bf16[1280,1280]{1,0:T(8,128)(2,1)}), bf16[1280,1280]{1,0:T(8,128)(2,1)}) %all-reduce.2.cloned.1.call-update) | async-done | bytes 3276816 | tf_op jit(solution)/shard_map/psum | solution.py:86
  173.5 5.2 %convert_element_type.124 = f32[1280,1280]{1,0:T(8,128)} convert(bf16[1280,1280]{1,0:T(8,128)(2,1)} %all-reduce.2.cloned.1.call-done) | non-fusion elementwise | flops 1638400 | bytes 9830400 | tf_op jit(solution)/shard_map/convert_element_type | solution.py:86
  178.7 38.6 %reduce-scatter.2.cloned.1.call-done = bf16[192,1280]{1,0:T(8,128)(2,1)} async-done(((bf16[768,1280]{1,0:T(8,128)(2,1)}), bf16[192,1280]{1,0:T(8,128)(2,1)}) %reduce-scatter.2.cloned.1.call-update) | async-done | bytes 491536 | tf_op jit(solution)/shard_map/reduce_scatter | solution.py:55
  217.4 0.0 copy-done.2
  217.4 0.0 copy-done.3
  217.4 2.2 fusion.66
  219.7 1.3 collective-permute-start
  221.0 4.5 %collective-permute-start.1 = (bf16[3,1280]{1,0:T(4,128)(2,1)S(1)}, bf16[3,1280]{1,0:T(4,128)(2,1)S(1)}, u32[]{:S(2)}, u32[]{:S(2)}) collective-permute-start(bf16[3,1280]{1,0:T(4,128)(2,1)S(1)} %get-tuple-element.24), channel_id=1, source_target_pairs={{0,1},{1,2},{2,3},{4,5},{5,6},{6,7},{8,9},{9,10},{10,11},{12,13},{... | collective-permute-start | bytes 23048 | tf_op jit(solution)/shard_map/ppermute | solution.py:17
  225.6 0.1 stack.31
  225.7 41.4 %psum.23 = f32[7,1280]{1,0:T(8,128)} all-reduce(f32[7,1280]{1,0:T(8,128)S(1)} %stack.31), channel_id=1, replica_groups=mesh['dp'=8,'tp'=4] {'dp','tp'}, use_global_device_ids=true, to_apply=%region_12.0 | all-reduce | flops 8960 | bytes 71680 | tf_op jit(solution)/shard_map/psum | solution.py:83
  267.0 0.0 collective-permute-done
  267.0 0.0 collective-permute-done.1
  267.0 1.7 fusion.76
  268.7 80.8 %all-gather.10.cloned.1.call-done = bf16[10240,1280]{1,0:T(8,128)(2,1)} async-done(((bf16[1280,1280]{1,0:T(8,128)(2,1)}), bf16[10240,1280]{1,0:T(8,128)(2,1)}) %all-gather.10.cloned.1.call-update) | async-done | bytes 26214416 | tf_op jit(solution)/shard_map/all_gather | solution.py:85
  349.5 0.0 copy-start.1
  349.5 20.1 %reduce_sum.87 = bf16[1280,1280]{1,0:T(8,128)(2,1)} reduce(bf16[8,1280,1280]{2,1,0:T(8,128)(2,1)} %bitcast.132, bf16[]{:T(256)} %constant.65.clone.1), dimensions={0}, to_apply=%region_1.0 | reduce | flops 11468800 | bytes 29491202 | tf_op jit(solution)/shard_map/reduce_sum | solution.py:85
  369.6 5.2 %convert_element_type.121 = f32[1280,1280]{1,0:T(8,128)} convert(bf16[1280,1280]{1,0:T(8,128)(2,1)} %reduce_sum.87) | non-fusion elementwise | flops 1638400 | bytes 9830400 | tf_op jit(solution)/shard_map/convert_element_type | solution.py:85
  374.8 0.0 copy-done.1
  (8 shorter events, 0.0 us)
Async XLA Ops:
  7.2 56.5 %copy-start = (bf16[1280,1280]{1,0:T(8,128)(2,1)S(1)}, bf16[1280,1280]{1,0:T(8,128)(2,1)}, u32[]{:S(2)}) copy-start(bf16[1280,1280]{1,0:T(8,128)(2,1)} %param.10) | copy-start | bytes 9830404
  7.2 48.6 %all-gather.8.cloned.1.call-start = ((), (), s32[]{:S(2)}) async-start(), calls=%async_computation.4 | async-start | bytes 2457600 | tf_op jit(solution)/shard_map/all_gather | solution.py:42
  7.9 92.4 %all-gather.6.cloned.1.call-start = ((), (), s32[]{:S(2)}) async-start(), calls=%async_computation.2 | async-start | bytes 2457600 | tf_op jit(solution)/shard_map/all_gather | solution.py:68
  8.9 7.5 %collective-permute-start.2 = (bf16[3,1280]{1,0:T(4,128)(2,1)S(1)}, bf16[3,1280]{1,0:T(4,128)(2,1)S(1)}, u32[]{:S(2)}, u32[]{:S(2)}) collective-permute-start(bf16[3,1280]{1,0:T(4,128)(2,1)S(1)} %get-tuple-element.25), channel_id=1, source_target_pairs={{0,1},{1,2},{2,3},{4,5},{5,6},{6,7},{8,9},{9,10},{10,11},{12,13},{... | collective-permute-start | bytes 23048 | tf_op jit(solution)/shard_map/ppermute | solution.py:17
  13.9 5.6 %collective-permute-start.3 = (bf16[3,1280]{1,0:T(4,128)(2,1)S(1)}, bf16[3,1280]{1,0:T(4,128)(2,1)S(1)}, u32[]{:S(2)}, u32[]{:S(2)}) collective-permute-start(bf16[3,1280]{1,0:T(4,128)(2,1)S(1)} %get-tuple-element.26), channel_id=1, source_target_pairs={{1,0},{2,1},{3,2},{5,4},{6,5},{7,6},{9,8},{10,9},{11,10},{13,12},{... | collective-permute-start | bytes 23048 | tf_op jit(solution)/shard_map/ppermute | solution.py:19
  23.8 149.7 %all-reduce.2.cloned.1.call-start = ((), (), s32[]{:S(2)}) async-start(), calls=%async_computation.3 | async-start | bytes 6553600 | tf_op jit(solution)/shard_map/psum | solution.py:86
  63.6 153.8 %reduce-scatter.2.cloned.1.call-start = ((), (), s32[]{:S(2)}) async-start(), calls=%async_computation.1 | async-start | bytes 2457600 | tf_op jit(solution)/shard_map/reduce_scatter | solution.py:55
  63.6 8.7 %copy-start.4 = (bf16[1280,1280]{1,0:T(8,128)(2,1)S(1)}, bf16[1280,1280]{1,0:T(8,128)(2,1)}, u32[]{:S(2)}) copy-start(bf16[1280,1280]{1,0:T(8,128)(2,1)} %param.9) | copy-start | bytes 9830404
  71.1 1.3 copy-start.5
  76.3 273.2 %all-gather.10.cloned.1.call-start = ((), (), s32[]{:S(2)}) async-start(), calls=%async_computation.5 | async-start | bytes 29491200 | tf_op jit(solution)/shard_map/all_gather | solution.py:85
  121.8 95.6 %copy-start.2 = (bf16[1,192,1280]{2,1,0:T(8,128)(2,1)S(1)}, bf16[1,192,1280]{2,1,0:T(8,128)(2,1)}, u32[]{:S(2)}) copy-start(bf16[1,192,1280]{2,1,0:T(8,128)(2,1)} %param.6) | copy-start | bytes 1474564
  121.8 95.6 %copy-start.3 = (bf16[1,192,1280]{2,1,0:T(8,128)(2,1)S(1)}, bf16[1,192,1280]{2,1,0:T(8,128)(2,1)}, u32[]{:S(2)}) copy-start(bf16[1,192,1280]{2,1,0:T(8,128)(2,1)} %param.8) | copy-start | bytes 1474564
  219.7 47.3 %collective-permute-start = (bf16[3,1280]{1,0:T(4,128)(2,1)S(1)}, bf16[3,1280]{1,0:T(4,128)(2,1)S(1)}, u32[]{:S(2)}, u32[]{:S(2)}) collective-permute-start(bf16[3,1280]{1,0:T(4,128)(2,1)S(1)} %get-tuple-element.23), channel_id=1, source_target_pairs={{1,0},{2,1},{3,2},{5,4},{6,5},{7,6},{9,8},{10,9},{11,10},{13,12},{... | collective-permute-start | bytes 23048 | tf_op jit(solution)/shard_map/ppermute | solution.py:19
  221.0 46.0 %collective-permute-start.1 = (bf16[3,1280]{1,0:T(4,128)(2,1)S(1)}, bf16[3,1280]{1,0:T(4,128)(2,1)S(1)}, u32[]{:S(2)}, u32[]{:S(2)}) collective-permute-start(bf16[3,1280]{1,0:T(4,128)(2,1)S(1)} %get-tuple-element.24), channel_id=1, source_target_pairs={{0,1},{1,2},{2,3},{4,5},{5,6},{6,7},{8,9},{9,10},{10,11},{12,13},{... | collective-permute-start | bytes 23048 | tf_op jit(solution)/shard_map/ppermute | solution.py:17
  349.5 25.3 %copy-start.1 = (bf16[1280,1280]{1,0:T(8,128)(2,1)S(1)}, bf16[1280,1280]{1,0:T(8,128)(2,1)}, u32[]{:S(2)}) copy-start(bf16[1280,1280]{1,0:T(8,128)(2,1)} %param.10) | copy-start | bytes 9830404
Sparse Core Ops, SparseCore 0:
  9.6 46.2 all-gather.7
  58.0 42.3 all-gather.5
  103.6 69.8 all-reduce.1
  175.7 41.6 reduce-scatter.1
  219.7 129.7 all-gather.9
